TPU v7x, 256 devices: a whole 4x4x8 slice. The times are simulated.
256 devices in a mesh: samples: 64 (over z, y, x_hi), snps: 4 (over x_lo, core).
Axes of the slice: x: 4 (x_hi: 2, x_lo: 2; x = x_hi * 2 + x_lo), y: 4, z: 8, core: 2. Of those that a mesh axis runs over, the one named last changes fastest.
Arguments:
- genotype: int32 [32768, 1536], P('samples', 'snps'), may hold values from 0 to 2
- mask: int32 [32768, 1536], P('samples', 'snps'), may hold values 0 or 1
Outputs:
- blocks: float32 [32768, 16896], P('samples', 'snps')
All inputs are finite; a program needn't handle non-finite values. No bound on the sum of `mask` on one device may be relied on, other than what follows from the above.
Results may differ from a plain program's by a relative error of at most 0.0014.
Values may be sent and summed in bfloat16 or wider, within the bound.
A program may use at most 128 MiB of HBM per device.

v0:
```python
import jax
import jax.numpy as jnp
from jax import lax
from jax.sharding import PartitionSpec as P


def sent_to_all(shard, axis):
    size = lax.axis_size(axis)
    return lax.all_to_all(
        jnp.broadcast_to(shard[None], (size, *shard.shape)), axis, 0, 0, tiled=True
    )


def over_copies(shard, axis):
    return sent_to_all(shard, axis).sum(axis=0)


def packed_total(arrays, axis):
    flat, at, gathered = (jnp.concatenate([a.reshape(-1) for a in arrays]), 0, [])
    running = over_copies(flat, axis)
    for a in arrays:
        gathered.append(running[at : at + a.size].reshape(a.shape))
        at += a.size
    return tuple(gathered)


def laid_out(pieces, dim):
    pieces = jnp.moveaxis(pieces, 0, dim)
    shape = pieces.shape
    return pieces.reshape(*shape[:dim], shape[dim] * shape[dim + 1], *shape[dim + 2 :])


def gather_directly(shard, axis, dim):
    pieces = sent_to_all(shard, axis)
    return laid_out(pieces, dim)


def passed_along(value, axis, steps):
    count = lax.axis_size(axis)
    pairs = [(source, (source + steps) % count) for source in range(count)]
    return lax.ppermute(value, axis, pairs)


def standardize(dosage, observed_mask, allele_sum, observed_sum):
    frequency = (allele_sum + 1.0) / (2.0 * observed_sum + 2.0)
    scaled = (
        observed_mask * (dosage - 2.0 * frequency) / jnp.sqrt(2.0 * frequency * (1.0 - frequency))
    )
    return scaled.astype(jnp.bfloat16)


def cross_block(own_rows, other_rows):
    return lax.dot_general(
        own_rows, other_rows, (((1,), (1,)), ((), ())), preferred_element_type=jnp.float32
    )


def place_block(target, block, offset):
    column = jnp.asarray(offset, jnp.int32) * block.shape[1]
    return lax.dynamic_update_slice(target, block, (jnp.int32(0), column))


def per_device(genotype, mask):
    dosage = genotype.astype(jnp.float32)
    observed_mask = mask.astype(jnp.float32)
    allele_sum, observed_sum = packed_total(
        (jnp.sum(dosage * observed_mask, axis=0), jnp.sum(observed_mask, axis=0)), "samples"
    )
    standard = standardize(dosage, observed_mask, allele_sum, observed_sum)
    circle_size = lax.axis_size("samples")
    snp_parts = lax.axis_size("snps")
    block_rows = standard.shape[0]
    offsets = circle_size // 2 + 1
    snp_total = standard.shape[1] * snp_parts
    wide_rows = gather_directly(standard, "snps", 1)
    part_index = lax.axis_index("snps")
    band_width = offsets * block_rows // snp_parts
    starts = [member * band_width // block_rows for member in range(snp_parts)]
    pieces = [standard]
    for member in range(1, snp_parts):
        pieces.append(passed_along(standard, "samples", -starts[member]))
    stacked = jnp.stack(pieces, axis=0)
    routed = lax.all_to_all(stacked, "snps", split_axis=0, concat_axis=2, tiled=True)
    holding = routed[0]
    first_block = part_index * band_width // block_rows
    count = -(-band_width // block_rows) + 1
    band = jnp.zeros((block_rows, count * block_rows), jnp.float32)
    band = place_block(band, cross_block(wide_rows, holding), 0)

    def walk_on(step_index, carry):
        band_now, current = carry
        current = passed_along(current, "samples", -1)
        return (place_block(band_now, cross_block(wide_rows, current), step_index), current)

    band, current_last = lax.fori_loop(1, count, walk_on, (band, holding))
    begin = part_index * band_width - first_block * block_rows
    return lax.dynamic_slice_in_dim(band, begin, band_width, 1) / snp_total


def solution(mesh):
    return jax.shard_map(
        per_device,
        mesh=mesh,
        in_specs=(P("samples", "snps"), P("samples", "snps")),
        out_specs=P("samples", "snps"),
        check_vma=False,
    )
```

profile of v0, /device:TPU:2, one launch (start us, length us, event | category | flops | bytes accessed | tf_op | source)
XLA Modules:
  0.0 500.0 jit_solution(16634381405950325777)
XLA Ops:
  0.0 1.6 multiply_reduce_fusion
  1.8 26.9 %all_to_all.26 = f32[64,1,768]{2,1,0:T(1,128)S(1)} all-to-all(f32[64,1,768]{2,1,0:T(1,128)S(1)} %broadcast_in_dim.6), channel_id=1, replica_groups=mesh['samples'=64,'snps'=4] {'samples'}, dimensions={0} | all-to-all | bytes 393216 | tf_op jit(solution)/shard_map/all_to_all | solution.py:9
  29.0 1.3 broadcast_in_dim.7
  30.3 5.0 all-to-all-start.1
  35.2 1.5 collective-permute-start.1
  37.4 3.4 collective-permute-start.3
  40.8 7.2 %collective-permute-done.1 = bf16[512,384]{1,0:T(8,128)(2,1)S(1)} collective-permute-done((bf16[512,384]{1,0:T(8,128)(2,1)S(1)}, bf16[512,384]{1,0:T(8,128)(2,1)S(1)}, u32[]{:S(2)}, u32[]{:S(2)}) %collective-permute-start.1) | collective-permute-done | bytes 393248 | tf_op jit(solution)/shard_map/ppermute | solution.py:41
  48.0 17.6 %collective-permute-done.2 = bf16[512,384]{1,0:T(8,128)(2,1)S(1)} collective-permute-done((bf16[512,384]{1,0:T(8,128)(2,1)S(1)}, bf16[512,384]{1,0:T(8,128)(2,1)S(1)}, u32[]{:S(2)}, u32[]{:S(2)}) %collective-permute-start.2) | collective-permute-done | bytes 393248 | tf_op jit(solution)/shard_map/ppermute | solution.py:41
  65.6 22.6 %collective-permute-done.3 = bf16[512,384]{1,0:T(8,128)(2,1)S(1)} collective-permute-done((bf16[512,384]{1,0:T(8,128)(2,1)S(1)}, bf16[512,384]{1,0:T(8,128)(2,1)S(1)}, u32[]{:S(2)}, u32[]{:S(2)}) %collective-permute-start.3) | collective-permute-done | bytes 393248 | tf_op jit(solution)/shard_map/ppermute | solution.py:41
  88.2 1.4 pad_maximum_fusion
  89.6 4.0 all-to-all-start.2
  93.6 1.6 copy.12
  95.2 2.6 copy.14
  97.8 14.2 %all-to-all-done.2 = bf16[4,512,384]{2,1,0:T(8,128)(2,1)S(1)} async-done(((bf16[4,512,384]{2,1,0:T(8,128)(2,1)}), bf16[4,512,384]{2,1,0:T(8,128)(2,1)S(1)}, u32[]{:S(2)}, u32[]{:S(2)}) %all-to-all-start.2) | async-done | bytes 1572896 | tf_op jit(solution)/shard_map/all_to_all | solution.py:83
  112.0 1.2 copy.13
  116.1 5.3 %dynamic_update_slice.10 = f32[512,5120]{1,0:T(8,128)} pad(f32[512,512]{1,0:T(8,128)S(1)} %fusion, f32[]{:T(128)} %constant.53.clone.1), padding=0_0x0_4608 | pad | bytes 11534340 | tf_op jit(solution)/shard_map/dynamic_update_slice | solution.py:60
  121.4 371.0 %while.15 = (s32[]{:T(128)}, f32[512,5120]{1,0:T(8,128)}, bf16[512,1536]{1,0:T(8,128)(2,1)}, bf16[512,1536]{1,0:T(8,128)(2,1)S(1)}, s32[]{:T(128)}, /*index=5*/s32[]{:T(128)}, s32[]{:T(128)}, s32[]{:T(128)}) while((s32[]{:T(128)}, f32[512,5120]{1,0:T(8,128)}, bf16[512,1536]{1,0:T(8,128)(2,1)}, bf16[512,1536]{1,0:T(8,128)(2,1)S(1)}, s32[]{:T(128)}, ...), condition=%wide.region_4.5_spmd, body=%wide.region_3.4_spmd.sunk | while | flops 805306368 | bytes 13631663 | solution.py:95
  121.4 2.0 collective-permute-start
  123.4 35.9 %collective-permute-done = bf16[512,1536]{1,0:T(8,128)(2,1)S(1)} collective-permute-done((bf16[512,1536]{1,0:T(8,128)(2,1)}, bf16[512,1536]{1,0:T(8,128)(2,1)S(1)}, u32[]{:S(2)}, u32[]{:S(2)}) %collective-permute-start) | collective-permute-done | bytes 1572896 | tf_op jit(solution)/shard_map/while/body/eval_jaxpr/ppermute | solution.py:41
  159.3 1.1 copy.28
  160.5 2.0 convolution_dynamic-update-slice_fusion.2
  162.5 6.2 %collective-permute-start = (bf16[512,1536]{1,0:T(8,128)(2,1)}, bf16[512,1536]{1,0:T(8,128)(2,1)S(1)}, u32[]{:S(2)}, u32[]{:S(2)}) collective-permute-start(bf16[512,1536]{1,0:T(8,128)(2,1)} %get-tuple-element.144), channel_id=1, source_target_pairs={{0,252},{4,0},{8,4},{12,8},{16,12},{20,16},{24,20},{28,24},{32,28}... | collective-permute-start | bytes 4718600 | tf_op jit(solution)/shard_map/while/body/eval_jaxpr/ppermute | solution.py:41
  168.7 33.2 %collective-permute-done = bf16[512,1536]{1,0:T(8,128)(2,1)S(1)} collective-permute-done((bf16[512,1536]{1,0:T(8,128)(2,1)}, bf16[512,1536]{1,0:T(8,128)(2,1)S(1)}, u32[]{:S(2)}, u32[]{:S(2)}) %collective-permute-start) | collective-permute-done | bytes 1572896 | tf_op jit(solution)/shard_map/while/body/eval_jaxpr/ppermute | solution.py:41
  201.9 1.1 copy.28
  203.1 2.0 convolution_dynamic-update-slice_fusion.2
  205.1 8.1 %collective-permute-start = (bf16[512,1536]{1,0:T(8,128)(2,1)}, bf16[512,1536]{1,0:T(8,128)(2,1)S(1)}, u32[]{:S(2)}, u32[]{:S(2)}) collective-permute-start(bf16[512,1536]{1,0:T(8,128)(2,1)} %get-tuple-element.144), channel_id=1, source_target_pairs={{0,252},{4,0},{8,4},{12,8},{16,12},{20,16},{24,20},{28,24},{32,28}... | collective-permute-start | bytes 4718600 | tf_op jit(solution)/shard_map/while/body/eval_jaxpr/ppermute | solution.py:41
  213.2 32.3 %collective-permute-done = bf16[512,1536]{1,0:T(8,128)(2,1)S(1)} collective-permute-done((bf16[512,1536]{1,0:T(8,128)(2,1)}, bf16[512,1536]{1,0:T(8,128)(2,1)S(1)}, u32[]{:S(2)}, u32[]{:S(2)}) %collective-permute-start) | collective-permute-done | bytes 1572896 | tf_op jit(solution)/shard_map/while/body/eval_jaxpr/ppermute | solution.py:41
  245.5 1.1 copy.28
  246.7 2.1 convolution_dynamic-update-slice_fusion.2
  248.7 8.1 %collective-permute-start = (bf16[512,1536]{1,0:T(8,128)(2,1)}, bf16[512,1536]{1,0:T(8,128)(2,1)S(1)}, u32[]{:S(2)}, u32[]{:S(2)}) collective-permute-start(bf16[512,1536]{1,0:T(8,128)(2,1)} %get-tuple-element.144), channel_id=1, source_target_pairs={{0,252},{4,0},{8,4},{12,8},{16,12},{20,16},{24,20},{28,24},{32,28}... | collective-permute-start | bytes 4718600 | tf_op jit(solution)/shard_map/while/body/eval_jaxpr/ppermute | solution.py:41
  256.8 31.5 %collective-permute-done = bf16[512,1536]{1,0:T(8,128)(2,1)S(1)} collective-permute-done((bf16[512,1536]{1,0:T(8,128)(2,1)}, bf16[512,1536]{1,0:T(8,128)(2,1)S(1)}, u32[]{:S(2)}, u32[]{:S(2)}) %collective-permute-start) | collective-permute-done | bytes 1572896 | tf_op jit(solution)/shard_map/while/body/eval_jaxpr/ppermute | solution.py:41
  289.4 2.0 convolution_dynamic-update-slice_fusion.2
  291.5 8.1 %collective-permute-start = (bf16[512,1536]{1,0:T(8,128)(2,1)}, bf16[512,1536]{1,0:T(8,128)(2,1)S(1)}, u32[]{:S(2)}, u32[]{:S(2)}) collective-permute-start(bf16[512,1536]{1,0:T(8,128)(2,1)} %get-tuple-element.144), channel_id=1, source_target_pairs={{0,252},{4,0},{8,4},{12,8},{16,12},{20,16},{24,20},{28,24},{32,28}... | collective-permute-start | bytes 4718600 | tf_op jit(solution)/shard_map/while/body/eval_jaxpr/ppermute | solution.py:41
  299.6 30.6 %collective-permute-done = bf16[512,1536]{1,0:T(8,128)(2,1)S(1)} collective-permute-done((bf16[512,1536]{1,0:T(8,128)(2,1)}, bf16[512,1536]{1,0:T(8,128)(2,1)S(1)}, u32[]{:S(2)}, u32[]{:S(2)}) %collective-permute-start) | collective-permute-done | bytes 1572896 | tf_op jit(solution)/shard_map/while/body/eval_jaxpr/ppermute | solution.py:41
  331.3 2.0 convolution_dynamic-update-slice_fusion.2
  333.4 8.1 %collective-permute-start = (bf16[512,1536]{1,0:T(8,128)(2,1)}, bf16[512,1536]{1,0:T(8,128)(2,1)S(1)}, u32[]{:S(2)}, u32[]{:S(2)}) collective-permute-start(bf16[512,1536]{1,0:T(8,128)(2,1)} %get-tuple-element.144), channel_id=1, source_target_pairs={{0,252},{4,0},{8,4},{12,8},{16,12},{20,16},{24,20},{28,24},{32,28}... | collective-permute-start | bytes 4718600 | tf_op jit(solution)/shard_map/while/body/eval_jaxpr/ppermute | solution.py:41
  341.5 29.7 %collective-permute-done = bf16[512,1536]{1,0:T(8,128)(2,1)S(1)} collective-permute-done((bf16[512,1536]{1,0:T(8,128)(2,1)}, bf16[512,1536]{1,0:T(8,128)(2,1)S(1)}, u32[]{:S(2)}, u32[]{:S(2)}) %collective-permute-start) | collective-permute-done | bytes 1572896 | tf_op jit(solution)/shard_map/while/body/eval_jaxpr/ppermute | solution.py:41
  372.4 2.0 convolution_dynamic-update-slice_fusion.2
  374.4 8.1 %collective-permute-start = (bf16[512,1536]{1,0:T(8,128)(2,1)}, bf16[512,1536]{1,0:T(8,128)(2,1)S(1)}, u32[]{:S(2)}, u32[]{:S(2)}) collective-permute-start(bf16[512,1536]{1,0:T(8,128)(2,1)} %get-tuple-element.144), channel_id=1, source_target_pairs={{0,252},{4,0},{8,4},{12,8},{16,12},{20,16},{24,20},{28,24},{32,28}... | collective-permute-start | bytes 4718600 | tf_op jit(solution)/shard_map/while/body/eval_jaxpr/ppermute | solution.py:41
  382.5 28.9 %collective-permute-done = bf16[512,1536]{1,0:T(8,128)(2,1)S(1)} collective-permute-done((bf16[512,1536]{1,0:T(8,128)(2,1)}, bf16[512,1536]{1,0:T(8,128)(2,1)S(1)}, u32[]{:S(2)}, u32[]{:S(2)}) %collective-permute-start) | collective-permute-done | bytes 1572896 | tf_op jit(solution)/shard_map/while/body/eval_jaxpr/ppermute | solution.py:41
  412.5 2.0 convolution_dynamic-update-slice_fusion.2
  414.6 8.1 %collective-permute-start = (bf16[512,1536]{1,0:T(8,128)(2,1)}, bf16[512,1536]{1,0:T(8,128)(2,1)S(1)}, u32[]{:S(2)}, u32[]{:S(2)}) collective-permute-start(bf16[512,1536]{1,0:T(8,128)(2,1)} %get-tuple-element.144), channel_id=1, source_target_pairs={{0,252},{4,0},{8,4},{12,8},{16,12},{20,16},{24,20},{28,24},{32,28}... | collective-permute-start | bytes 4718600 | tf_op jit(solution)/shard_map/while/body/eval_jaxpr/ppermute | solution.py:41
  422.7 28.0 %collective-permute-done = bf16[512,1536]{1,0:T(8,128)(2,1)S(1)} collective-permute-done((bf16[512,1536]{1,0:T(8,128)(2,1)}, bf16[512,1536]{1,0:T(8,128)(2,1)S(1)}, u32[]{:S(2)}, u32[]{:S(2)}) %collective-permute-start) | collective-permute-done | bytes 1572896 | tf_op jit(solution)/shard_map/while/body/eval_jaxpr/ppermute | solution.py:41
  451.9 2.0 convolution_dynamic-update-slice_fusion.2
  453.9 8.1 %collective-permute-start = (bf16[512,1536]{1,0:T(8,128)(2,1)}, bf16[512,1536]{1,0:T(8,128)(2,1)S(1)}, u32[]{:S(2)}, u32[]{:S(2)}) collective-permute-start(bf16[512,1536]{1,0:T(8,128)(2,1)} %get-tuple-element.144), channel_id=1, source_target_pairs={{0,252},{4,0},{8,4},{12,8},{16,12},{20,16},{24,20},{28,24},{32,28}... | collective-permute-start | bytes 4718600 | tf_op jit(solution)/shard_map/while/body/eval_jaxpr/ppermute | solution.py:41
  462.0 27.2 %collective-permute-done = bf16[512,1536]{1,0:T(8,128)(2,1)S(1)} collective-permute-done((bf16[512,1536]{1,0:T(8,128)(2,1)}, bf16[512,1536]{1,0:T(8,128)(2,1)S(1)}, u32[]{:S(2)}, u32[]{:S(2)}) %collective-permute-start) | collective-permute-done | bytes 1572896 | tf_op jit(solution)/shard_map/while/body/eval_jaxpr/ppermute | solution.py:41
  490.3 2.0 convolution_dynamic-update-slice_fusion.2
  492.4 7.7 %dynamic-slice_multiply_fusion = f32[512,4224]{1,0:T(8,128)} fusion(f32[512,5120]{1,0:T(8,128)} %get-tuple-element.84, s32[]{:T(128)S(6)} %select_n.16), kind=kLoop, calls=%fused_computation.1 | loop fusion | flops 2162688 | bytes 17301508 | tf_op jit(solution)/shard_map/div | solution.py:97
  (26 shorter events, 10.9 us)
Async XLA Ops:
  0.0 28.8 %copy-start.1 = (s32[512,384]{1,0:T(8,128)S(1)}, s32[512,384]{1,0:T(8,128)}, u32[]{:S(2)}) copy-start(s32[512,384]{1,0:T(8,128)} %param.4) | copy-start | bytes 2359300
  0.0 28.8 %copy-start.2 = (s32[512,384]{1,0:T(8,128)S(1)}, s32[512,384]{1,0:T(8,128)}, u32[]{:S(2)}) copy-start(s32[512,384]{1,0:T(8,128)} %param.5) | copy-start | bytes 2359300
  30.3 59.3 %all-to-all-start.1 = ((bf16[4,512,384]{2,1,0:T(8,128)(2,1)}), bf16[4,512,384]{2,1,0:T(8,128)(2,1)S(1)}, u32[]{:S(2)}, u32[]{:S(2)}) async-start(bf16[4,512,384]{2,1,0:T(8,128)(2,1)} %broadcast_in_dim.7), calls=%async_computation.1 | async-start | bytes 3145728 | tf_op jit(solution)/shard_map/all_to_all | solution.py:9
  35.2 12.8 %collective-permute-start.1 = (bf16[512,384]{1,0:T(8,128)(2,1)S(1)}, bf16[512,384]{1,0:T(8,128)(2,1)S(1)}, u32[]{:S(2)}, u32[]{:S(2)}) collective-permute-start(bf16[512,384]{1,0:T(8,128)(2,1)S(1)} %divide_convert_fusion), channel_id=1, source_target_pairs={{0,224},{4,228},{8,232},{12,236},{16,240},{20,244},{24,248},{28,25... | collective-permute-start | bytes 1179656 | tf_op jit(solution)/shard_map/ppermute | solution.py:41
  36.8 28.8 %collective-permute-start.2 = (bf16[512,384]{1,0:T(8,128)(2,1)S(1)}, bf16[512,384]{1,0:T(8,128)(2,1)S(1)}, u32[]{:S(2)}, u32[]{:S(2)}) collective-permute-start(bf16[512,384]{1,0:T(8,128)(2,1)S(1)} %divide_convert_fusion), channel_id=1, source_target_pairs={{0,192},{4,196},{8,200},{12,204},{16,208},{20,212},{24,216},{28,22... | collective-permute-start | bytes 1179656 | tf_op jit(solution)/shard_map/ppermute | solution.py:41
  37.4 50.8 %collective-permute-start.3 = (bf16[512,384]{1,0:T(8,128)(2,1)S(1)}, bf16[512,384]{1,0:T(8,128)(2,1)S(1)}, u32[]{:S(2)}, u32[]{:S(2)}) collective-permute-start(bf16[512,384]{1,0:T(8,128)(2,1)S(1)} %divide_convert_fusion), channel_id=1, source_target_pairs={{0,160},{4,164},{8,168},{12,172},{16,176},{20,180},{24,184},{28,18... | collective-permute-start | bytes 1179656 | tf_op jit(solution)/shard_map/ppermute | solution.py:41
  89.6 22.4 %all-to-all-start.2 = ((bf16[4,512,384]{2,1,0:T(8,128)(2,1)}), bf16[4,512,384]{2,1,0:T(8,128)(2,1)S(1)}, u32[]{:S(2)}, u32[]{:S(2)}) async-start(bf16[4,512,384]{2,1,0:T(8,128)(2,1)} %pad_maximum_fusion), calls=%async_computation.2 | async-start | bytes 3145728 | tf_op jit(solution)/shard_map/all_to_all | solution.py:83
  113.2 1.9 copy-start
  113.5 1.1 copy-start.4
  116.1 5.3 %copy-start.3 = (bf16[512,1536]{1,0:T(8,128)(2,1)S(1)}, bf16[512,1536]{1,0:T(8,128)(2,1)}, u32[]{:S(2)}) copy-start(bf16[512,1536]{1,0:T(8,128)(2,1)} %copy.14) | copy-start | bytes 4718596
  121.4 37.9 %collective-permute-start = (bf16[512,1536]{1,0:T(8,128)(2,1)}, bf16[512,1536]{1,0:T(8,128)(2,1)S(1)}, u32[]{:S(2)}, u32[]{:S(2)}) collective-permute-start(bf16[512,1536]{1,0:T(8,128)(2,1)} %get-tuple-element.144), channel_id=1, source_target_pairs={{0,252},{4,0},{8,4},{12,8},{16,12},{20,16},{24,20},{28,24},{32,28}... | collective-permute-start | bytes 4718600 | tf_op jit(solution)/shard_map/while/body/eval_jaxpr/ppermute | solution.py:41
  162.5 39.4 %collective-permute-start = (bf16[512,1536]{1,0:T(8,128)(2,1)}, bf16[512,1536]{1,0:T(8,128)(2,1)S(1)}, u32[]{:S(2)}, u32[]{:S(2)}) collective-permute-start(bf16[512,1536]{1,0:T(8,128)(2,1)} %get-tuple-element.144), channel_id=1, source_target_pairs={{0,252},{4,0},{8,4},{12,8},{16,12},{20,16},{24,20},{28,24},{32,28}... | collective-permute-start | bytes 4718600 | tf_op jit(solution)/shard_map/while/body/eval_jaxpr/ppermute | solution.py:41
  205.1 40.4 %collective-permute-start = (bf16[512,1536]{1,0:T(8,128)(2,1)}, bf16[512,1536]{1,0:T(8,128)(2,1)S(1)}, u32[]{:S(2)}, u32[]{:S(2)}) collective-permute-start(bf16[512,1536]{1,0:T(8,128)(2,1)} %get-tuple-element.144), channel_id=1, source_target_pairs={{0,252},{4,0},{8,4},{12,8},{16,12},{20,16},{24,20},{28,24},{32,28}... | collective-permute-start | bytes 4718600 | tf_op jit(solution)/shard_map/while/body/eval_jaxpr/ppermute | solution.py:41
  248.7 39.6 %collective-permute-start = (bf16[512,1536]{1,0:T(8,128)(2,1)}, bf16[512,1536]{1,0:T(8,128)(2,1)S(1)}, u32[]{:S(2)}, u32[]{:S(2)}) collective-permute-start(bf16[512,1536]{1,0:T(8,128)(2,1)} %get-tuple-element.144), channel_id=1, source_target_pairs={{0,252},{4,0},{8,4},{12,8},{16,12},{20,16},{24,20},{28,24},{32,28}... | collective-permute-start | bytes 4718600 | tf_op jit(solution)/shard_map/while/body/eval_jaxpr/ppermute | solution.py:41
  291.5 38.7 %collective-permute-start = (bf16[512,1536]{1,0:T(8,128)(2,1)}, bf16[512,1536]{1,0:T(8,128)(2,1)S(1)}, u32[]{:S(2)}, u32[]{:S(2)}) collective-permute-start(bf16[512,1536]{1,0:T(8,128)(2,1)} %get-tuple-element.144), channel_id=1, source_target_pairs={{0,252},{4,0},{8,4},{12,8},{16,12},{20,16},{24,20},{28,24},{32,28}... | collective-permute-start | bytes 4718600 | tf_op jit(solution)/shard_map/while/body/eval_jaxpr/ppermute | solution.py:41
  333.4 37.9 %collective-permute-start = (bf16[512,1536]{1,0:T(8,128)(2,1)}, bf16[512,1536]{1,0:T(8,128)(2,1)S(1)}, u32[]{:S(2)}, u32[]{:S(2)}) collective-permute-start(bf16[512,1536]{1,0:T(8,128)(2,1)} %get-tuple-element.144), channel_id=1, source_target_pairs={{0,252},{4,0},{8,4},{12,8},{16,12},{20,16},{24,20},{28,24},{32,28}... | collective-permute-start | bytes 4718600 | tf_op jit(solution)/shard_map/while/body/eval_jaxpr/ppermute | solution.py:41
  374.4 37.0 %collective-permute-start = (bf16[512,1536]{1,0:T(8,128)(2,1)}, bf16[512,1536]{1,0:T(8,128)(2,1)S(1)}, u32[]{:S(2)}, u32[]{:S(2)}) collective-permute-start(bf16[512,1536]{1,0:T(8,128)(2,1)} %get-tuple-element.144), channel_id=1, source_target_pairs={{0,252},{4,0},{8,4},{12,8},{16,12},{20,16},{24,20},{28,24},{32,28}... | collective-permute-start | bytes 4718600 | tf_op jit(solution)/shard_map/while/body/eval_jaxpr/ppermute | solution.py:41
  414.6 36.1 %collective-permute-start = (bf16[512,1536]{1,0:T(8,128)(2,1)}, bf16[512,1536]{1,0:T(8,128)(2,1)S(1)}, u32[]{:S(2)}, u32[]{:S(2)}) collective-permute-start(bf16[512,1536]{1,0:T(8,128)(2,1)} %get-tuple-element.144), channel_id=1, source_target_pairs={{0,252},{4,0},{8,4},{12,8},{16,12},{20,16},{24,20},{28,24},{32,28}... | collective-permute-start | bytes 4718600 | tf_op jit(solution)/shard_map/while/body/eval_jaxpr/ppermute | solution.py:41
  453.9 35.3 %collective-permute-start = (bf16[512,1536]{1,0:T(8,128)(2,1)}, bf16[512,1536]{1,0:T(8,128)(2,1)S(1)}, u32[]{:S(2)}, u32[]{:S(2)}) collective-permute-start(bf16[512,1536]{1,0:T(8,128)(2,1)} %get-tuple-element.144), channel_id=1, source_target_pairs={{0,252},{4,0},{8,4},{12,8},{16,12},{20,16},{24,20},{28,24},{32,28}... | collective-permute-start | bytes 4718600 | tf_op jit(solution)/shard_map/while/body/eval_jaxpr/ppermute | solution.py:41
where the time goes:
time: 500 us
  waiting for transfers between devices  339 us (68%)
  starting transfers between devices  79.4 us (16%)
  blocking collectives  26.9 us (5%)
  local copies, waits for them, and re-layouts  24.3 us (5%)
  matrix products  19.4 us (4%)
  other arithmetic  11.1 us (2%)
    ppermute x12, waiting for transfers between devices, passed_along(): return lax.ppermute(value, axis, pairs)  325 us
    ppermute x12, starting transfers between devices, passed_along(): return lax.ppermute(value, axis, pairs)  70.5 us
    all_to_all x1, blocking collectives, sent_to_all(): lax.all_to_all(jnp.broadcast_to(shard[None], (size, *shard.shape)), axis,...  26.9 us
    dot_general x10, matrix products, cross_block(): lax.dot_general(own_rows, other_rows, (((1,), (1,)), ((), ())), preferred...  19.4 us
    all_to_all x1, waiting for transfers between devices, per_device(): lax.all_to_all(stacked, 'snps', split_axis=0, concat_axis=2, tiled=True)  14.2 us
    while x9, local copies, waits for them, and re-layouts  10.3 us
  transfers between devices with their start and end apart: 14, of which 13 were waited for; matrix products, arithmetic and copies ran while one was open for 1% of the time, Pallas kernels for 0%

commit v1 on v0

v1 whole, which is shorter than its diff:
```python
import jax
import jax.numpy as jnp
from jax import lax
from jax.experimental import pallas as pl
from jax.experimental.pallas import tpu as pltpu
from jax.sharding import PartitionSpec as P

MESH = pl.DeviceIdType.MESH
Y = 4
R = 8
SLOTS = 5
TILE = 256


def sent_to_all(shard, axis):
    size = lax.axis_size(axis)
    return lax.all_to_all(
        jnp.broadcast_to(shard[None], (size, *shard.shape)), axis, 0, 0, tiled=True
    )


def packed_total(arrays, axis):
    flat = jnp.concatenate([a.reshape(-1) for a in arrays])
    running = sent_to_all(flat, axis).sum(axis=0)
    half = flat.shape[0] // 2
    return running[:half], running[half:]


def standardize(dosage, observed_mask, allele_sum, observed_sum):
    frequency = (allele_sum + 1.0) / (2.0 * observed_sum + 2.0)
    scaled = (
        observed_mask * (dosage - 2.0 * frequency) / jnp.sqrt(2.0 * frequency * (1.0 - frequency))
    )
    return scaled.astype(jnp.bfloat16)


def exchange_kernel(z_size, std, out, slots, lhs, stage, recv, recv_piece, recv_lhs, send, local_sem, out_sem):
    rows, width = std.shape
    total = 4 * width
    pair = 2 * rows
    chunk = rows // R
    i = lax.axis_index("samples")
    m = lax.axis_index("snps")
    xh, q = i % 2, i // 2
    y, z = q % Y, q // Y
    core, xl = m % 2, m // 2
    mine, theirs = xh, 1 - xh

    def at(dz, dy, half, member):
        zz = lax.rem(z + dz + z_size, z_size)
        yy = lax.rem(y + dy + Y, Y)
        return ((zz * Y + yy) * 2 + half, member)

    def span(slot, parity, r):
        return pl.ds(pl.multiple_of(slot * pair + parity * rows + r * chunk, chunk), chunk)

    def columns(member):
        return pl.ds(pl.multiple_of(member * width, width), width)

    def forward(stream, source, slot, parity, r, device):
        pltpu.make_async_remote_copy(
            src_ref=slots.at[span(source, parity, r)],
            dst_ref=slots.at[span(slot, parity, r)],
            send_sem=send.at[stream],
            recv_sem=recv.at[slot, parity, r],
            device_id=device,
            device_id_type=MESH,
        ).start()

    def arrived(slot, parity, r):
        pltpu.make_async_copy(
            slots.at[span(slot, parity, r)], slots.at[span(slot, parity, r)], recv.at[slot, parity, r]
        ).wait()

    def drained(stream, count):
        pltpu.make_async_copy(
            slots.at[pl.ds(0, count)], slots.at[pl.ds(0, count)], send.at[stream]
        ).wait()

    ring = [(h, k) for h in range(2) for k in range(4)]
    barrier = pltpu.get_barrier_semaphore()
    peers = []
    for dh in range(2):
        for dm in range(4):
            if dh or dm:
                peers.append(at(0, 0, lax.rem(xh + dh, 2), lax.rem(m + dm, 4)))
    for dz in (-1, 1):
        for c in range(2):
            peers.append(at(dz, 0, xh, xl * 2 + c))
    for dy in (-1, 1):
        peers.append(at(0, dy, xh, m))
    for peer in peers:
        pl.semaphore_signal(barrier, inc=1, device_id=peer, device_id_type=MESH)
    pl.semaphore_wait(barrier, len(peers))

    own_rows = pl.ds(pl.multiple_of(xh * rows, rows), rows)
    to_slot = pltpu.make_async_copy(std, slots.at[own_rows, columns(0)], local_sem)
    to_lhs = pltpu.make_async_copy(std, lhs.at[:, columns(m)], local_sem)

    @pl.when(m == 0)
    def _():
        to_slot.start()

    @pl.when(m != 0)
    def _():
        to_lhs.start()

        def piece(r, carry):
            pltpu.make_async_remote_copy(
                src_ref=std.at[pl.ds(pl.multiple_of(r * chunk, chunk), chunk)],
                dst_ref=slots.at[span(0, xh, r), columns(m)],
                send_sem=send.at[0],
                recv_sem=recv_piece.at[m, r],
                device_id=at(0, 0, xh, 0),
                device_id_type=MESH,
            ).start()
            return carry

        lax.fori_loop(0, R, piece, 0)

    def lhs_copy(dm):
        member = lax.rem(m + dm, 4)
        return pltpu.make_async_remote_copy(
            src_ref=std,
            dst_ref=lhs.at[:, columns(m)],
            send_sem=send.at[dm],
            recv_sem=recv_lhs.at[m],
            device_id=at(0, 0, xh, member),
            device_id_type=MESH,
        )

    def send_lhs():
        for dm in range(1, 4):
            @pl.when(lax.rem(m + dm, 4) != 0)
            def _():
                lhs_copy(dm).start()

    def both_ways(source, parity, r):
        forward(6, source, 3, parity, r, at(0, 1, xh, m))
        forward(7, source, 1, parity, r, at(0, -1, xh, m))

    def guarded(r, body):
        pl.when((r >= 0) & (r < R))(lambda: body(r))

    @pl.when(core == 0)
    def _():
        @pl.when(m == 0)
        def _():
            to_slot.wait()

        def own(r):
            @pl.when(xl == 0)
            def _():
                for member in range(1, 4):
                    pltpu.make_async_copy(
                        slots.at[span(0, xh, r), columns(member)],
                        slots.at[span(0, xh, r), columns(member)],
                        recv_piece.at[member, r],
                    ).wait()
                forward(4, 0, 0, mine, r, at(0, 0, 1 - xh, m))

            @pl.when(xl == 1)
            def _():
                arrived(0, mine, r)

            forward(5, 0, 0, mine, r, at(-1, 0, xh, m + 1))
            pl.when(y == Y - 1)(lambda: both_ways(0, mine, r))

        def other(r):
            arrived(0, theirs, r)
            pl.when(y == Y - 1)(lambda: both_ways(0, theirs, r))

        def last(r):
            for parity in (mine, theirs):
                arrived(4, parity, r)
                pl.when(y == 0)(lambda: both_ways(4, parity, r))

        def step(t, carry):
            guarded(t, own)
            guarded(t - 1, other)
            guarded(t - 2, last)
            return carry

        lax.fori_loop(0, R + 2, step, 0)
        send_lhs()

        def finish(r, carry):
            for slot in (1, 3, 2):
                for parity in (mine, theirs):
                    arrived(slot, parity, r)
            return carry

        lax.fori_loop(0, R, finish, 0)
        pl.when(xl == 0)(lambda: drained(4, rows))
        drained(5, rows)

        @pl.when((y == 0) | (y == Y - 1))
        def _():
            drained(6, pair)
            drained(7, pair)

    @pl.when(core == 1)
    def _():
        def first_out(parity, r):
            forward(6, 0, 4, parity, r, at(0, 0, xh, m - 1))
            pl.when(y > 0)(lambda: forward(8, 0, 1, parity, r, at(0, -1, xh, m)))
            pl.when(y == Y - 1)(lambda: forward(9, 0, 3, parity, r, at(0, 1, xh, m)))

        def last_out(parity, r):
            pl.when(y < Y - 1)(lambda: forward(9, 4, 3, parity, r, at(0, 1, xh, m)))
            pl.when(y == 0)(lambda: forward(8, 4, 1, parity, r, at(0, -1, xh, m)))

        def first_own(r):
            arrived(0, mine, r)
            forward(5, 0, 4, mine, r, at(-1, 0, xh, m))
            forward(4, 0, 0, mine, r, at(0, 0, 1 - xh, m))
            first_out(mine, r)

        def first_other(r):
            arrived(0, theirs, r)
            first_out(theirs, r)

        def last_own(r):
            arrived(4, mine, r)

            @pl.when(xl == 0)
            def _():
                forward(10, 4, 0, mine, r, at(0, 0, 0, 2))
                forward(11, 4, 0, mine, r, at(0, 0, 1, 2))

            forward(7, 4, 4, mine, r, at(0, 0, 1 - xh, m))
            last_out(mine, r)

        def last_other(r):
            arrived(4, theirs, r)
            last_out(theirs, r)

        def sides(r):
            for parity in (mine, theirs):
                arrived(1, parity, r)
                pl.when(y < 2)(lambda: forward(12, 1, 1, parity, r, at(1, 0, xh, m - 1)))
                pl.when((y == 1) | (y == 2))(lambda: forward(14, 1, 2, parity, r, at(0, -1, xh, m)))
                arrived(3, parity, r)
                pl.when(y >= 2)(lambda: forward(12, 3, 3, parity, r, at(1, 0, xh, m - 1)))
                pl.when((y == 1) | (y == 2))(lambda: forward(15, 3, 2, parity, r, at(0, 1, xh, m)))

        def middle(r):
            for parity in (mine, theirs):
                arrived(2, parity, r)
                forward(13, 2, 2, parity, r, at(1, 0, xh, m - 1))

        def step(t, carry):
            guarded(t, first_own)
            guarded(t - 1, first_other)
            guarded(t - 1, last_own)
            guarded(t - 2, last_other)
            guarded(t - 3, sides)
            guarded(t - 6, middle)
            return carry

        lax.fori_loop(0, R + 6, step, 0)
        send_lhs()
        for stream in (4, 5, 7):
            drained(stream, rows)
        for stream in (6, 8, 9, 12, 13):
            drained(stream, pair)

        @pl.when(xl == 0)
        def _():
            drained(10, rows)
            drained(11, rows)

        @pl.when((y == 1) | (y == 2))
        def _():
            drained(14, pair)
            drained(15, pair)

    @pl.when(m != 0)
    def _():
        to_lhs.wait()
        whole = std.at[:]
        pltpu.make_async_copy(whole, whole, send.at[0]).wait()
        for dm in range(1, 4):
            pltpu.make_async_copy(
                lhs.at[:, columns(lax.rem(m + dm, 4))],
                lhs.at[:, columns(lax.rem(m + dm, 4))],
                recv_lhs.at[lax.rem(m + dm, 4)],
            ).wait()

    for dm in range(1, 4):
        @pl.when(lax.rem(m + dm, 4) != 0)
        def _():
            lhs_copy(dm).wait_send()

    @pl.when(m == 0)
    def _():
        lhs[...] = slots[own_rows, :]

    begin = pl.multiple_of(xh * rows + m * (rows // 4), rows // 4)
    band = out.shape[1]

    def product(start, size):
        return lax.dot_general(
            lhs[...],
            slots[pl.ds(pl.multiple_of(begin + start, rows // 4), size), :],
            (((1,), (1,)), ((), ())),
            preferred_element_type=jnp.float32,
        )

    def to_out(k, slot):
        return pltpu.make_async_copy(
            stage.at[slot], out.at[:, pl.ds(pl.multiple_of(k * TILE, TILE), TILE)], out_sem.at[slot]
        )

    tiles = band // TILE

    def tile_step(k, carry):
        slot = lax.rem(k, 2)
        pl.when(k >= 2)(lambda: to_out(k - 2, slot).wait())
        stage[slot] = product(k * TILE, TILE)
        to_out(k, slot).start()
        return carry

    lax.fori_loop(0, tiles, tile_step, 0)
    to_out(tiles - 2, tiles % 2).wait()
    rest = band - tiles * TILE
    stage[tiles % 2, :, :rest] = product(tiles * TILE, rest)
    tail = pltpu.make_async_copy(
        stage.at[tiles % 2, :, pl.ds(0, rest)], out.at[:, pl.ds(tiles * TILE, rest)], out_sem.at[tiles % 2]
    )
    tail.start()
    to_out(tiles - 1, (tiles - 1) % 2).wait()
    tail.wait()


def per_device(genotype, mask):
    dosage = genotype.astype(jnp.float32)
    observed_mask = mask.astype(jnp.float32)
    allele_sum, observed_sum = packed_total(
        (jnp.sum(dosage * observed_mask, axis=0), jnp.sum(observed_mask, axis=0)), "samples"
    )
    standard = standardize(dosage, observed_mask, allele_sum, observed_sum)
    circle = lax.axis_size("samples")
    rows, width = standard.shape
    parts = lax.axis_size("snps")
    band = (circle // 2 + 1) * rows // parts
    total = width * parts

    def kernel(*refs):
        exchange_kernel(circle // (2 * Y), *refs)

    sums = pl.pallas_call(
        kernel,
        out_shape=jax.ShapeDtypeStruct((rows, band), jnp.float32),
        in_specs=[pl.BlockSpec(memory_space=pl.ANY)],
        out_specs=pl.BlockSpec(memory_space=pl.ANY),
        scratch_shapes=[
            pltpu.VMEM((SLOTS * 2 * rows, total), jnp.bfloat16),
            pltpu.VMEM((rows, total), jnp.bfloat16),
            pltpu.VMEM((2, rows, TILE), jnp.float32),
            pltpu.SemaphoreType.DMA((SLOTS, 2, R)),
            pltpu.SemaphoreType.DMA((4, R)),
            pltpu.SemaphoreType.DMA((4,)),
            pltpu.SemaphoreType.DMA((16,)),
            pltpu.SemaphoreType.DMA,
            pltpu.SemaphoreType.DMA((2,)),
        ],
        compiler_params=pltpu.CompilerParams(
            collective_id=0, has_side_effects=True, vmem_limit_bytes=48 * 1024 * 1024
        ),
        cost_estimate=pl.CostEstimate(
            flops=2 * rows * band * total, bytes_accessed=rows * band * 4, transcendentals=0
        ),
    )(standard)
    return sums / total


def solution(mesh):
    return jax.shard_map(
        per_device,
        mesh=mesh,
        in_specs=(P("samples", "snps"), P("samples", "snps")),
        out_specs=P("samples", "snps"),
        check_vma=False,
    )
```

time: 500 us -> 186 us (0.37)
  waiting for transfers between devices: 339 us -> 0 us
  Pallas kernels: 0 us -> 147 us
  starting transfers between devices: 79.4 us -> 0 us
  local copies, waits for them, and re-layouts: 24.3 us -> 0.11 us
  matrix products: 19.4 us -> 0 us
    ppermute x12 -> x0, waiting for transfers between devices: 325 us -> none  [passed_along(): return lax.ppermute(value, axis, pairs)]
    pallas_call x0 -> x1, Pallas kernels: none -> 147 us  [per_device(): pl.pallas_call(kernel, out_shape=jax.ShapeDtypeStruct((rows, band), jnp.f...]
    ppermute x12 -> x0, starting transfers between devices: 70.5 us -> none  [passed_along(): return lax.ppermute(value, axis, pairs)]
    dot_general x10 -> x0, matrix products: 19.4 us -> none  [cross_block(): lax.dot_general(own_rows, other_rows, (((1,), (1,)), ((), ())), preferred...]
    all_to_all x2 -> x0, waiting for transfers between devices: 14.2 us -> none  [the longest x1 14.2 us: per_device(): lax.all_to_all(stacked, 'snps', split_axis=0, concat_axis=2, tiled=True)]
    while x10 -> x0, local copies, waits for them, and re-layouts: 13 us -> none
    all_to_all x2 -> x0, starting transfers between devices: 8.96 us -> none  [the longest x1 4.97 us: sent_to_all(): lax.all_to_all(jnp.broadcast_to(shard[None], (size, *shard.shape)), axis,...]
    dynamic_update_slice x1 -> x0, local copies, waits for them, and re-layouts: 5.25 us -> none  [place_block(): return lax.dynamic_update_slice(target, block, (jnp.int32(0), column))]
  transfers between devices with their start and end apart: 14 -> 0, of which waited for: 13 -> 0; matrix products, arithmetic and copies ran while one was open for 1% -> 0% of each run, Pallas kernels for 0% -> 0%
where the time goes in v1:
time: 186 us; the launch traced here: 184 us
  Pallas kernels  147 us (79%)
  blocking collectives  26.9 us (14%)
  other arithmetic  10.9 us (6%)
    pallas_call x1, Pallas kernels, per_device(): pl.pallas_call(kernel, out_shape=jax.ShapeDtypeStruct((rows, band), jnp.f...  147 us
    all_to_all x1, blocking collectives, sent_to_all(): lax.all_to_all(jnp.broadcast_to(shard[None], (size, *shard.shape)), axis,...  26.9 us
    div x1, other arithmetic, per_device(): return sums / total  7.68 us

profile of v1, /device:TPU:2, one launch (start us, length us, event | category | flops | bytes accessed | tf_op | source)
XLA Modules:
  0.0 184.4 jit_solution(1099822489674567908)
XLA Ops:
  0.0 1.5 multiply_reduce_fusion
  1.5 0.1 broadcast_in_dim.2
  1.7 26.9 %all_to_all.6 = f32[64,1,768]{2,1,0:T(1,128)S(1)} all-to-all(f32[64,1,768]{2,1,0:T(1,128)S(1)} %broadcast_in_dim.2), channel_id=1, replica_groups=mesh['samples'=64,'snps'=4] {'samples'}, dimensions={0} | all-to-all | bytes 393216 | tf_op jit(solution)/shard_map/all_to_all | solution.py:17
  28.5 0.1 reduce_sum.29
  28.7 1.5 divide_convert_fusion.refs_0_
  30.2 146.5 %shard_map.28 = f32[512,4224]{1,0:T(8,128)} custom-call(bf16[512,384]{1,0:T(8,128)(2,1)S(1)} %divide_convert_fusion.refs_0_), custom_call_target="tpu_custom_call" | custom-call | flops 6643777536 | bytes 8650752 | tf_op jit(solution)/shard_map/pallas_call | solution.py:352
  176.7 7.7 %broadcast_multiply_fusion = f32[512,4224]{1,0:T(8,128)} fusion(f32[512,4224]{1,0:T(8,128)} %shard_map.28), kind=kLoop, calls=%fused_computation | loop fusion | flops 2162688 | bytes 17301504 | tf_op jit(solution)/shard_map/div | solution.py:375
  (3 shorter events, 0.0 us)

commit v2 on v1

--- a/solution.py
+++ b/solution.py
@@ -7,23 +7,10 @@
 
 MESH = pl.DeviceIdType.MESH
 Y = 4
-R = 8
+R = 16
 SLOTS = 5
-TILE = 256
-
-
-def sent_to_all(shard, axis):
-    size = lax.axis_size(axis)
-    return lax.all_to_all(
-        jnp.broadcast_to(shard[None], (size, *shard.shape)), axis, 0, 0, tiled=True
-    )
-
-
-def packed_total(arrays, axis):
-    flat = jnp.concatenate([a.reshape(-1) for a in arrays])
-    running = sent_to_all(flat, axis).sum(axis=0)
-    half = flat.shape[0] // 2
-    return running[:half], running[half:]
+UNIT = 128
+VMEM_MIB = 24
 
 
 def standardize(dosage, observed_mask, allele_sum, observed_sum):
@@ -34,7 +21,10 @@
     return scaled.astype(jnp.bfloat16)
 
 
-def exchange_kernel(z_size, std, out, slots, lhs, stage, recv, recv_piece, recv_lhs, send, local_sem, out_sem):
+def exchange_kernel(
+    z_size, genotype, mask, out,
+    std, slots, lhs, plane, column, recv, recv_piece, recv_lhs, recv_count, send, send_count,
+):
     rows, width = std.shape
     total = 4 * width
     pair = 2 * rows
@@ -45,6 +35,7 @@
     y, z = q % Y, q // Y
     core, xl = m % 2, m // 2
     mine, theirs = xh, 1 - xh
+    band = out.shape[1]
 
     def at(dz, dy, half, member):
         zz = lax.rem(z + dz + z_size, z_size)
@@ -89,22 +80,70 @@
             peers.append(at(dz, 0, xh, xl * 2 + c))
     for dy in (-1, 1):
         peers.append(at(0, dy, xh, m))
-    for peer in peers:
+    here = y * 2 + xh
+    crowd = []
+    for d in range(1, 2 * Y):
+        other = lax.rem(here + d, 2 * Y)
+        crowd.append((i - here + other, m))
+    tower = [at(d, 0, xh, m) for d in range(1, z_size)]
+    everyone = peers + crowd + tower
+    for peer in everyone:
         pl.semaphore_signal(barrier, inc=1, device_id=peer, device_id_type=MESH)
-    pl.semaphore_wait(barrier, len(peers))
-
+
+    def counted(ref_a, ref_b):
+        dosage, seen = ref_a[...].astype(jnp.float32), ref_b[...].astype(jnp.float32)
+        return (
+            jnp.sum(dosage * seen, axis=0, keepdims=True),
+            jnp.sum(seen, axis=0, keepdims=True),
+        )
+
+    alleles, observed = counted(genotype, mask)
+    line = lax.broadcasted_iota(jnp.int32, (8, width), 0)
+    plane[here] = jnp.where(line == 0, alleles, jnp.where(line == 1, observed, 0.0))
+    pl.semaphore_wait(barrier, len(everyone))
+
+    def share(buffer, index, phase, devices, size):
+        copies = [
+            pltpu.make_async_remote_copy(
+                src_ref=buffer.at[index],
+                dst_ref=buffer.at[index],
+                send_sem=send_count.at[phase, d],
+                recv_sem=recv_count.at[phase, index],
+                device_id=device,
+                device_id_type=MESH,
+            )
+            for d, device in enumerate(devices)
+        ]
+        for copy in copies:
+            copy.start()
+        for d in range(1, size):
+            source = lax.rem(index + d, size)
+            pltpu.make_async_copy(
+                buffer.at[source], buffer.at[source], recv_count.at[phase, source]
+            ).wait()
+        return copies
+
+    sent = share(plane, here, 0, crowd, 2 * Y)
+    column[z] = jnp.sum(plane[...], axis=0)
+    sent += share(column, z, 1, tower, z_size)
+    counts = jnp.sum(column[...], axis=0)
+    standard = standardize(
+        genotype[...].astype(jnp.float32), mask[...].astype(jnp.float32), counts[0:1], counts[1:2]
+    )
+    std[...] = standard
     own_rows = pl.ds(pl.multiple_of(xh * rows, rows), rows)
-    to_slot = pltpu.make_async_copy(std, slots.at[own_rows, columns(0)], local_sem)
-    to_lhs = pltpu.make_async_copy(std, lhs.at[:, columns(m)], local_sem)
 
     @pl.when(m == 0)
     def _():
-        to_slot.start()
+        slots[own_rows, 0:width] = standard
+
+    for member in range(1, 4):
+        @pl.when(m == member)
+        def _():
+            lhs[:, member * width : (member + 1) * width] = standard
 
     @pl.when(m != 0)
     def _():
-        to_lhs.start()
-
         def piece(r, carry):
             pltpu.make_async_remote_copy(
                 src_ref=std.at[pl.ds(pl.multiple_of(r * chunk, chunk), chunk)],
@@ -118,22 +157,64 @@
 
         lax.fori_loop(0, R, piece, 0)
 
-    def lhs_copy(dm):
-        member = lax.rem(m + dm, 4)
+    def lhs_copy(stream, source, owner, member):
         return pltpu.make_async_remote_copy(
-            src_ref=std,
-            dst_ref=lhs.at[:, columns(m)],
-            send_sem=send.at[dm],
-            recv_sem=recv_lhs.at[m],
+            src_ref=source,
+            dst_ref=lhs.at[:, columns(owner)],
+            send_sem=send.at[stream],
+            recv_sem=recv_lhs.at[owner],
             device_id=at(0, 0, xh, member),
             device_id_type=MESH,
         )
 
-    def send_lhs():
-        for dm in range(1, 4):
-            @pl.when(lax.rem(m + dm, 4) != 0)
-            def _():
-                lhs_copy(dm).start()
+    mate = jnp.where(m < 2, m + 2, 5 - m)
+    lhs_copy(1, std, m, mate).start()
+    pl.when(m != 1)(lambda: lhs_copy(2, std, m, 1).start())
+
+    def lhs_wait(owner):
+        pltpu.make_async_copy(
+            lhs.at[:, columns(owner)], lhs.at[:, columns(owner)], recv_lhs.at[owner]
+        ).wait()
+
+    def pass_lhs():
+        @pl.when(m >= 2)
+        def _():
+            lhs_wait(m - 2)
+            lhs_copy(3, lhs.at[:, columns(m - 2)], m - 2, 5 - m).start()
+
+    def lhs_ready():
+        @pl.when(m == 0)
+        def _():
+            lhs[...] = slots[own_rows, :]
+
+        @pl.when(m == 1)
+        def _():
+            for owner in (0, 2, 3):
+                lhs_wait(owner)
+
+        @pl.when(m >= 2)
+        def _():
+            lhs_wait(5 - m)
+            lhs_wait(3 - m)
+
+    begin = xh * 4 + m
+
+    def product(unit, count):
+        first = pl.multiple_of(unit * UNIT, UNIT)
+        out[:, pl.ds(pl.multiple_of((unit - begin) * UNIT, UNIT), count * UNIT)] = lax.dot_general(
+            lhs[...],
+            slots[pl.ds(first, count * UNIT), :],
+            (((1,), (1,)), ((), ())),
+            preferred_element_type=jnp.float32,
+        )
+
+    def tile(slot, parity, half):
+        unit = slot * (pair // UNIT) + parity * (rows // UNIT) + half * 2
+        low = unit - begin
+        units = band // UNIT
+        pl.when((low >= 0) & (low < units - 1))(lambda: product(unit, 2))
+        pl.when(low == -1)(lambda: product(unit + 1, 1))
+        pl.when(low == units - 1)(lambda: product(unit, 1))
 
     def both_ways(source, parity, r):
         forward(6, source, 3, parity, r, at(0, 1, xh, m))
@@ -144,10 +225,6 @@
 
     @pl.when(core == 0)
     def _():
-        @pl.when(m == 0)
-        def _():
-            to_slot.wait()
-
         def own(r):
             @pl.when(xl == 0)
             def _():
@@ -179,18 +256,25 @@
             guarded(t, own)
             guarded(t - 1, other)
             guarded(t - 2, last)
+            pl.when(t == 1)(pass_lhs)
             return carry
 
         lax.fori_loop(0, R + 2, step, 0)
-        send_lhs()
-
-        def finish(r, carry):
-            for slot in (1, 3, 2):
+        lhs_ready()
+
+        def finish(half, carry):
+            for slot in (0, 4, 1, 3, 2):
                 for parity in (mine, theirs):
-                    arrived(slot, parity, r)
+                    if slot in (1, 2, 3):
+                        def chunks(r, c):
+                            arrived(slot, parity, half * (R // 2) + r)
+                            return c
+
+                        lax.fori_loop(0, R // 2, chunks, 0)
+                    tile(slot, parity, half)
             return carry
 
-        lax.fori_loop(0, R, finish, 0)
+        lax.fori_loop(0, 2, finish, 0)
         pl.when(xl == 0)(lambda: drained(4, rows))
         drained(5, rows)
 
@@ -249,17 +333,30 @@
                 arrived(2, parity, r)
                 forward(13, 2, 2, parity, r, at(1, 0, xh, m - 1))
 
+        def early_tile(k, half):
+            slot = jnp.where(k < 2, 0, jnp.where(k < 4, 4, jnp.where(k < 6, 1, jnp.where(k < 8, 3, 2))))
+            tile(slot, jnp.where(k % 2 == 0, mine, theirs), half)
+
         def step(t, carry):
             guarded(t, first_own)
             guarded(t - 1, first_other)
             guarded(t - 1, last_own)
             guarded(t - 2, last_other)
             guarded(t - 3, sides)
-            guarded(t - 6, middle)
+            guarded(t - 4, middle)
+
+            pl.when(t == 1)(pass_lhs)
+            pl.when(t == R // 2)(lhs_ready)
+            pl.when((t >= R // 2) & (t < R // 2 + 10))(lambda: early_tile(t - R // 2, 0))
             return carry
 
-        lax.fori_loop(0, R + 6, step, 0)
-        send_lhs()
+        lax.fori_loop(0, R + 4, step, 0)
+
+        def late(k, carry):
+            early_tile(k, 1)
+            return carry
+
+        lax.fori_loop(0, 10, late, 0)
         for stream in (4, 5, 7):
             drained(stream, rows)
         for stream in (6, 8, 9, 12, 13):
@@ -275,103 +372,50 @@
             drained(14, pair)
             drained(15, pair)
 
-    @pl.when(m != 0)
-    def _():
-        to_lhs.wait()
-        whole = std.at[:]
-        pltpu.make_async_copy(whole, whole, send.at[0]).wait()
-        for dm in range(1, 4):
-            pltpu.make_async_copy(
-                lhs.at[:, columns(lax.rem(m + dm, 4))],
-                lhs.at[:, columns(lax.rem(m + dm, 4))],
-                recv_lhs.at[lax.rem(m + dm, 4)],
-            ).wait()
-
-    for dm in range(1, 4):
-        @pl.when(lax.rem(m + dm, 4) != 0)
-        def _():
-            lhs_copy(dm).wait_send()
-
-    @pl.when(m == 0)
-    def _():
-        lhs[...] = slots[own_rows, :]
-
-    begin = pl.multiple_of(xh * rows + m * (rows // 4), rows // 4)
-    band = out.shape[1]
-
-    def product(start, size):
-        return lax.dot_general(
-            lhs[...],
-            slots[pl.ds(pl.multiple_of(begin + start, rows // 4), size), :],
-            (((1,), (1,)), ((), ())),
-            preferred_element_type=jnp.float32,
-        )
-
-    def to_out(k, slot):
-        return pltpu.make_async_copy(
-            stage.at[slot], out.at[:, pl.ds(pl.multiple_of(k * TILE, TILE), TILE)], out_sem.at[slot]
-        )
-
-    tiles = band // TILE
-
-    def tile_step(k, carry):
-        slot = lax.rem(k, 2)
-        pl.when(k >= 2)(lambda: to_out(k - 2, slot).wait())
-        stage[slot] = product(k * TILE, TILE)
-        to_out(k, slot).start()
-        return carry
-
-    lax.fori_loop(0, tiles, tile_step, 0)
-    to_out(tiles - 2, tiles % 2).wait()
-    rest = band - tiles * TILE
-    stage[tiles % 2, :, :rest] = product(tiles * TILE, rest)
-    tail = pltpu.make_async_copy(
-        stage.at[tiles % 2, :, pl.ds(0, rest)], out.at[:, pl.ds(tiles * TILE, rest)], out_sem.at[tiles % 2]
-    )
-    tail.start()
-    to_out(tiles - 1, (tiles - 1) % 2).wait()
-    tail.wait()
+    for copy in sent:
+        copy.wait_send()
+    lhs_copy(1, std, m, mate).wait_send()
+    pl.when(m != 1)(lambda: lhs_copy(2, std, m, 1).wait_send())
+    pl.when(m >= 2)(lambda: lhs_copy(3, std, m - 2, 5 - m).wait_send())
+    pl.when(m != 0)(lambda: pltpu.make_async_copy(std, std, send.at[0]).wait())
 
 
 def per_device(genotype, mask):
-    dosage = genotype.astype(jnp.float32)
-    observed_mask = mask.astype(jnp.float32)
-    allele_sum, observed_sum = packed_total(
-        (jnp.sum(dosage * observed_mask, axis=0), jnp.sum(observed_mask, axis=0)), "samples"
-    )
-    standard = standardize(dosage, observed_mask, allele_sum, observed_sum)
     circle = lax.axis_size("samples")
-    rows, width = standard.shape
+    rows, width = genotype.shape
     parts = lax.axis_size("snps")
     band = (circle // 2 + 1) * rows // parts
     total = width * parts
+    z_size = circle // (2 * Y)
 
     def kernel(*refs):
-        exchange_kernel(circle // (2 * Y), *refs)
+        exchange_kernel(z_size, *refs)
 
     sums = pl.pallas_call(
         kernel,
         out_shape=jax.ShapeDtypeStruct((rows, band), jnp.float32),
-        in_specs=[pl.BlockSpec(memory_space=pl.ANY)],
-        out_specs=pl.BlockSpec(memory_space=pl.ANY),
+        in_specs=[pl.BlockSpec(memory_space=pltpu.VMEM)] * 2,
+        out_specs=pl.BlockSpec(memory_space=pltpu.VMEM),
         scratch_shapes=[
+            pltpu.VMEM((rows, width), jnp.bfloat16),
             pltpu.VMEM((SLOTS * 2 * rows, total), jnp.bfloat16),
             pltpu.VMEM((rows, total), jnp.bfloat16),
-            pltpu.VMEM((2, rows, TILE), jnp.float32),
+            pltpu.VMEM((2 * Y, 8, width), jnp.float32),
+            pltpu.VMEM((z_size, 8, width), jnp.float32),
             pltpu.SemaphoreType.DMA((SLOTS, 2, R)),
             pltpu.SemaphoreType.DMA((4, R)),
             pltpu.SemaphoreType.DMA((4,)),
+            pltpu.SemaphoreType.DMA((2, max(z_size, 2 * Y))),
             pltpu.SemaphoreType.DMA((16,)),
-            pltpu.SemaphoreType.DMA,
-            pltpu.SemaphoreType.DMA((2,)),
+            pltpu.SemaphoreType.DMA((2, max(z_size, 2 * Y))),
         ],
         compiler_params=pltpu.CompilerParams(
-            collective_id=0, has_side_effects=True, vmem_limit_bytes=48 * 1024 * 1024
+            collective_id=0, has_side_effects=True, vmem_limit_bytes=VMEM_MIB * 1024 * 1024
         ),
         cost_estimate=pl.CostEstimate(
             flops=2 * rows * band * total, bytes_accessed=rows * band * 4, transcendentals=0
         ),
-    )(standard)
+    )(genotype, mask)
     return sums / total
 
 

time: 186 us -> 135 us (0.73)
  blocking collectives: 26.9 us -> 0 us
  Pallas kernels: 147 us -> 128 us
  other arithmetic: 10.9 us -> 4.23 us
  local copies, waits for them, and re-layouts: 0.11 us -> 2.27 us
    all_to_all x1 -> x0, blocking collectives: 26.9 us -> none  [sent_to_all(): lax.all_to_all(jnp.broadcast_to(shard[None], (size, *shard.shape)), axis,...]
    pallas_call x1, Pallas kernels: 147 us -> 128 us  [per_device(): pl.pallas_call(kernel, out_shape=jax.ShapeDtypeStruct((rows, band), jnp.f...]
    div x1, other arithmetic: 7.68 us -> 4.23 us  [per_device(): return sums / total]
    unnamed x0 -> x4, local copies, waits for them, and re-layouts: none -> 2.27 us
where the time goes in v2:
time: 135 us; the launch traced here: 134 us
  Pallas kernels  128 us (95%)
  other arithmetic  4.23 us (3%)
  local copies, waits for them, and re-layouts  2.27 us (2%)
    pallas_call x1, Pallas kernels, per_device(): pl.pallas_call(kernel, out_shape=jax.ShapeDtypeStruct((rows, band), jnp.f...  128 us
    div x1, other arithmetic, per_device(): return sums / total  4.23 us

profile of v2, /device:TPU:2, one launch (start us, length us, event | category | flops | bytes accessed | tf_op | source)
XLA Modules:
  0.0 134.5 jit_solution(14622836560016361649)
XLA Ops:
  0.0 0.0 copy-start
  0.0 1.1 copy-done
  1.1 0.0 copy-start.1
  1.1 1.1 copy-done.1
  2.3 128.0 %shard_map.28 = f32[512,4224]{1,0:T(8,128)S(1)} custom-call(s32[512,384]{1,0:T(8,128)S(1)} %copy-done, s32[512,384]{1,0:T(8,128)S(1)} %copy-done.1), custom_call_target="tpu_custom_call" | custom-call | flops 6643777536 | bytes 8650752 | tf_op jit(solution)/shard_map/pallas_call | solution.py:394
  130.3 4.2 %broadcast_multiply_fusion = f32[512,4224]{1,0:T(8,128)} fusion(f32[512,4224]{1,0:T(8,128)S(1)} %shard_map.28), kind=kLoop, calls=%fused_computation | loop fusion | flops 2162688 | bytes 17301504 | tf_op jit(solution)/shard_map/div | solution.py:419
Async XLA Ops:
  0.0 1.1 copy-start
  1.1 1.1 copy-start.1

commit v3 on v2

--- a/solution.py
+++ b/solution.py
@@ -10,19 +10,24 @@
 R = 16
 SLOTS = 5
 UNIT = 128
-VMEM_MIB = 24
-
-
-def standardize(dosage, observed_mask, allele_sum, observed_sum):
+DOUBLED = (3, 3)
+CROSSED = (3, 2)
+MID_CROSSED = (0, 4)
+FIRST_DOWN = (4, 3)
+LAST_DOWN = (4, 2)
+LAG_EVEN = ((0, 2, 12), (0, 2, 15))
+LAG_ODD = ((0, 1, 4, 5, 7), (0, 2, 4, 4, 6))
+VMEM_MIB = 30
+
+
+def levels(allele_sum, observed_sum):
     frequency = (allele_sum + 1.0) / (2.0 * observed_sum + 2.0)
-    scaled = (
-        observed_mask * (dosage - 2.0 * frequency) / jnp.sqrt(2.0 * frequency * (1.0 - frequency))
-    )
-    return scaled.astype(jnp.bfloat16)
+    spread = jnp.sqrt(2.0 * frequency * (1.0 - frequency))
+    return [(dosage - 2.0 * frequency) / spread for dosage in (0.0, 1.0, 2.0)]
 
 
 def exchange_kernel(
-    z_size, genotype, mask, out,
+    z_size, call, out,
     std, slots, lhs, plane, column, recv, recv_piece, recv_lhs, recv_count, send, send_count,
 ):
     rows, width = std.shape
@@ -68,7 +73,6 @@
             slots.at[pl.ds(0, count)], slots.at[pl.ds(0, count)], send.at[stream]
         ).wait()
 
-    ring = [(h, k) for h in range(2) for k in range(4)]
     barrier = pltpu.get_barrier_semaphore()
     peers = []
     for dh in range(2):
@@ -90,16 +94,18 @@
     for peer in everyone:
         pl.semaphore_signal(barrier, inc=1, device_id=peer, device_id_type=MESH)
 
-    def counted(ref_a, ref_b):
-        dosage, seen = ref_a[...].astype(jnp.float32), ref_b[...].astype(jnp.float32)
-        return (
-            jnp.sum(dosage * seen, axis=0, keepdims=True),
-            jnp.sum(seen, axis=0, keepdims=True),
-        )
-
-    alleles, observed = counted(genotype, mask)
-    line = lax.broadcasted_iota(jnp.int32, (8, width), 0)
-    plane[here] = jnp.where(line == 0, alleles, jnp.where(line == 1, observed, 0.0))
+    value = call[...].astype(jnp.float32)
+    lanes = width // 3
+    sums = (
+        jnp.sum(jnp.maximum(value - 1.0, 0.0), axis=0, keepdims=True),
+        jnp.sum(jnp.minimum(value, 1.0), axis=0, keepdims=True),
+    )
+    line = lax.broadcasted_iota(jnp.int32, (8, lanes), 0)
+    packed = jnp.zeros((8, lanes), jnp.float32)
+    for k in range(6):
+        part = sums[k // 3][:, (k % 3) * lanes : (k % 3 + 1) * lanes]
+        packed = jnp.where(line == k, part, packed)
+    plane[here] = packed
     pl.semaphore_wait(barrier, len(everyone))
 
     def share(buffer, index, phase, devices, size):
@@ -127,9 +133,12 @@
     column[z] = jnp.sum(plane[...], axis=0)
     sent += share(column, z, 1, tower, z_size)
     counts = jnp.sum(column[...], axis=0)
-    standard = standardize(
-        genotype[...].astype(jnp.float32), mask[...].astype(jnp.float32), counts[0:1], counts[1:2]
+    alleles, observed = (
+        jnp.concatenate([counts[3 * k + n : 3 * k + n + 1] for n in range(3)], axis=1) for k in range(2)
     )
+    low, middle_level, high = levels(alleles, observed)
+    seen = jnp.where(value == 1.0, low, jnp.where(value == 2.0, middle_level, high))
+    standard = jnp.where(value == 0.0, 0.0, seen).astype(jnp.bfloat16)
     std[...] = standard
     own_rows = pl.ds(pl.multiple_of(xh * rows, rows), rows)
 
@@ -206,7 +215,7 @@
             slots[pl.ds(first, count * UNIT), :],
             (((1,), (1,)), ((), ())),
             preferred_element_type=jnp.float32,
-        )
+        ) / total
 
     def tile(slot, parity, half):
         unit = slot * (pair // UNIT) + parity * (rows // UNIT) + half * 2
@@ -216,17 +225,65 @@
         pl.when(low == -1)(lambda: product(unit + 1, 1))
         pl.when(low == units - 1)(lambda: product(unit, 1))
 
+    def by_half(values):
+        return values[0] if values[0] == values[1] else jnp.where(xl == 0, values[0], values[1])
+
+    def marked(shares, shift, r):
+        return lax.rem(r + shift, 4) < by_half(shares)
+
+    def doubled(r):
+        return marked(DOUBLED, 0, r)
+
+    def crossed(r):
+        return marked(CROSSED, 1, r)
+
+    def mid_crossed(r):
+        return marked(MID_CROSSED, 2, r)
+
+    def guarded(n, body):
+        @pl.when((n >= 0) & (n < 2 * R))
+        def _():
+            own = n < R
+            body(own, jnp.where(own, mine, theirs), lax.rem(n, R))
+
     def both_ways(source, parity, r):
         forward(6, source, 3, parity, r, at(0, 1, xh, m))
         forward(7, source, 1, parity, r, at(0, -1, xh, m))
 
-    def guarded(r, body):
-        pl.when((r >= 0) & (r < R))(lambda: body(r))
+    def tiles_of(k, group, start=0, stop=4):
+        j, phase = lax.rem(k, R // 2), k // (R // 2)
+
+        @pl.when((k >= 0) & (phase >= start) & (phase < stop) & (j < len(group)))
+        def _():
+            slot = jnp.int32(group[-1])
+            for place, value in enumerate(group[:-1]):
+                slot = jnp.where(j == place, value, slot)
+            tile(slot, jnp.where(phase < 2, mine, theirs), lax.rem(phase, 2))
+
+    def tile_step(t, early, late, whole):
+        pl.when(t == early + (R if whole else R // 2))(lhs_ready)
+        tiles_of(t - early - R // 2, (0, 4), start=int(whole))
+        if whole:
+            tiles_of(t - early - R - 2, (0, 4), stop=1)
+        tiles_of(t - late - R // 2, (1, 3, 2))
+
+    def settle(stream, count):
+        for half in range(2):
+            if count(half):
+                pl.when(xl == half)(lambda: drained(stream, chunk * count(half)))
+
+    def tally(shares, shift):
+        return lambda half: [int((r + shift) % 4 < shares[half]) for r in range(R)]
+
+    is_doubled, is_crossed, is_mid = tally(DOUBLED, 0), tally(CROSSED, 1), tally(MID_CROSSED, 2)
+    is_first, is_last = tally(FIRST_DOWN, 3), tally(LAST_DOWN, 1)
+    steps = 2 * R
+    side = jnp.where(y < 2, 3, 1)
 
     @pl.when(core == 0)
     def _():
-        def own(r):
-            @pl.when(xl == 0)
+        def first(own, parity, r):
+            @pl.when(own & (xl == 0))
             def _():
                 for member in range(1, 4):
                     pltpu.make_async_copy(
@@ -236,141 +293,131 @@
                     ).wait()
                 forward(4, 0, 0, mine, r, at(0, 0, 1 - xh, m))
 
-            @pl.when(xl == 1)
+            @pl.when(jnp.logical_not(own & (xl == 0)))
             def _():
-                arrived(0, mine, r)
-
-            forward(5, 0, 0, mine, r, at(-1, 0, xh, m + 1))
-            pl.when(y == Y - 1)(lambda: both_ways(0, mine, r))
-
-        def other(r):
-            arrived(0, theirs, r)
-            pl.when(y == Y - 1)(lambda: both_ways(0, theirs, r))
-
-        def last(r):
-            for parity in (mine, theirs):
-                arrived(4, parity, r)
-                pl.when(y == 0)(lambda: both_ways(4, parity, r))
+                arrived(0, parity, r)
+
+            pl.when(own | marked(FIRST_DOWN, 3, r))(
+                lambda: forward(5, 0, 0, parity, r, at(-1, 0, xh, m + 1))
+            )
+            pl.when((y == Y - 1) & doubled(r))(lambda: both_ways(0, parity, r))
+
+        def last(own, parity, r):
+            arrived(4, parity, r)
+            pl.when((y == 0) & doubled(r))(lambda: both_ways(4, parity, r))
+
+        def sides(own, parity, r):
+            for slot in (1, 3, 2):
+                arrived(slot, parity, r)
+                by_ring = doubled(r) & (side == slot)
+                pl.when(own & crossed(r) & jnp.logical_not(by_ring))(
+                    lambda: forward(8, slot, slot, parity, r, at(0, 0, 1 - xh, m))
+                )
+
+        lag = [by_half(v) for v in zip(*LAG_EVEN)]
 
         def step(t, carry):
-            guarded(t, own)
-            guarded(t - 1, other)
-            guarded(t - 2, last)
+            guarded(t - lag[0], first)
+            guarded(t - lag[1], last)
+            guarded(t - lag[2], sides)
             pl.when(t == 1)(pass_lhs)
+            tile_step(t, jnp.maximum(lag[0], lag[1]), lag[2], True)
             return carry
 
-        lax.fori_loop(0, R + 2, step, 0)
-        lhs_ready()
-
-        def finish(half, carry):
-            for slot in (0, 4, 1, 3, 2):
-                for parity in (mine, theirs):
-                    if slot in (1, 2, 3):
-                        def chunks(r, c):
-                            arrived(slot, parity, half * (R // 2) + r)
-                            return c
-
-                        lax.fori_loop(0, R // 2, chunks, 0)
-                    tile(slot, parity, half)
-            return carry
-
-        lax.fori_loop(0, 2, finish, 0)
+        lax.fori_loop(0, steps + max(max(v[0], v[1] + 2, v[2] + 3) for v in LAG_EVEN), step, 0)
         pl.when(xl == 0)(lambda: drained(4, rows))
-        drained(5, rows)
+        settle(5, lambda half: R + sum(is_first(half)))
+        settle(8, lambda half: sum(c * (3 - d) for c, d in zip(is_crossed(half), is_doubled(half))))
 
         @pl.when((y == 0) | (y == Y - 1))
         def _():
-            drained(6, pair)
-            drained(7, pair)
+            settle(6, lambda half: 2 * sum(is_doubled(half)))
+            settle(7, lambda half: 2 * sum(is_doubled(half)))
 
     @pl.when(core == 1)
     def _():
-        def first_out(parity, r):
+        def first(own, parity, r):
+            arrived(0, parity, r)
+            pl.when(own | marked(LAST_DOWN, 1, r))(
+                lambda: forward(5, 0, 4, parity, r, at(-1, 0, xh, m))
+            )
+            pl.when(own & jnp.logical_not(marked(FIRST_DOWN, 3, r)))(
+                lambda: forward(4, 0, 0, parity, r, at(0, 0, 1 - xh, m))
+            )
             forward(6, 0, 4, parity, r, at(0, 0, xh, m - 1))
             pl.when(y > 0)(lambda: forward(8, 0, 1, parity, r, at(0, -1, xh, m)))
             pl.when(y == Y - 1)(lambda: forward(9, 0, 3, parity, r, at(0, 1, xh, m)))
 
-        def last_out(parity, r):
+        def last(own, parity, r):
+            arrived(4, parity, r)
+
+            @pl.when(own & (xl == 0))
+            def _():
+                forward(10, 4, 0, parity, r, at(0, 0, 0, 2))
+                forward(11, 4, 0, parity, r, at(0, 0, 1, 2))
+
+            pl.when(own & jnp.logical_not(marked(LAST_DOWN, 1, r)))(
+                lambda: forward(7, 4, 4, parity, r, at(0, 0, 1 - xh, m))
+            )
             pl.when(y < Y - 1)(lambda: forward(9, 4, 3, parity, r, at(0, 1, xh, m)))
             pl.when(y == 0)(lambda: forward(8, 4, 1, parity, r, at(0, -1, xh, m)))
 
-        def first_own(r):
-            arrived(0, mine, r)
-            forward(5, 0, 4, mine, r, at(-1, 0, xh, m))
-            forward(4, 0, 0, mine, r, at(0, 0, 1 - xh, m))
-            first_out(mine, r)
-
-        def first_other(r):
-            arrived(0, theirs, r)
-            first_out(theirs, r)
-
-        def last_own(r):
-            arrived(4, mine, r)
-
-            @pl.when(xl == 0)
-            def _():
-                forward(10, 4, 0, mine, r, at(0, 0, 0, 2))
-                forward(11, 4, 0, mine, r, at(0, 0, 1, 2))
-
-            forward(7, 4, 4, mine, r, at(0, 0, 1 - xh, m))
-            last_out(mine, r)
-
-        def last_other(r):
-            arrived(4, theirs, r)
-            last_out(theirs, r)
-
-        def sides(r):
-            for parity in (mine, theirs):
-                arrived(1, parity, r)
-                pl.when(y < 2)(lambda: forward(12, 1, 1, parity, r, at(1, 0, xh, m - 1)))
-                pl.when((y == 1) | (y == 2))(lambda: forward(14, 1, 2, parity, r, at(0, -1, xh, m)))
-                arrived(3, parity, r)
-                pl.when(y >= 2)(lambda: forward(12, 3, 3, parity, r, at(1, 0, xh, m - 1)))
-                pl.when((y == 1) | (y == 2))(lambda: forward(15, 3, 2, parity, r, at(0, 1, xh, m)))
-
-        def middle(r):
-            for parity in (mine, theirs):
-                arrived(2, parity, r)
-                forward(13, 2, 2, parity, r, at(1, 0, xh, m - 1))
-
-        def early_tile(k, half):
-            slot = jnp.where(k < 2, 0, jnp.where(k < 4, 4, jnp.where(k < 6, 1, jnp.where(k < 8, 3, 2))))
-            tile(slot, jnp.where(k % 2 == 0, mine, theirs), half)
+        def relay(slot, own, parity, r):
+            by_ring = doubled(r) & (side == slot)
+            pl.when(jnp.logical_not(by_ring) & (own | jnp.logical_not(crossed(r))))(
+                lambda: forward(12, slot, slot, parity, r, at(1, 0, xh, m - 1))
+            )
+
+        def toward(stream, slot, dy, own, parity, r):
+            inner = (y == 1) | (y == 2)
+            pl.when(inner & (own | jnp.logical_not(mid_crossed(r))))(
+                lambda: forward(stream, slot, 2, parity, r, at(0, dy, xh, m))
+            )
+
+        def low_side(own, parity, r):
+            arrived(1, parity, r)
+            relay(1, own, parity, r)
+            toward(14, 1, -1, own, parity, r)
+
+        def high_side(own, parity, r):
+            arrived(3, parity, r)
+            relay(3, own, parity, r)
+            toward(15, 3, 1, own, parity, r)
+
+        def middle(own, parity, r):
+            arrived(2, parity, r)
+            relay(2, own, parity, r)
+            pl.when(own & mid_crossed(r))(
+                lambda: forward(13, 2, 2, parity, r, at(0, 0, 1 - xh, m))
+            )
+
+        lag = [by_half(v) for v in zip(*LAG_ODD)]
 
         def step(t, carry):
-            guarded(t, first_own)
-            guarded(t - 1, first_other)
-            guarded(t - 1, last_own)
-            guarded(t - 2, last_other)
-            guarded(t - 3, sides)
-            guarded(t - 4, middle)
-
+            guarded(t - lag[0], first)
+            guarded(t - lag[1], last)
+            guarded(t - lag[2], low_side)
+            guarded(t - lag[3], high_side)
+            guarded(t - lag[4], middle)
             pl.when(t == 1)(pass_lhs)
-            pl.when(t == R // 2)(lhs_ready)
-            pl.when((t >= R // 2) & (t < R // 2 + 10))(lambda: early_tile(t - R // 2, 0))
+            tile_step(t, jnp.maximum(lag[0], lag[1]), lag[4], False)
             return carry
 
-        lax.fori_loop(0, R + 4, step, 0)
-
-        def late(k, carry):
-            early_tile(k, 1)
-            return carry
-
-        lax.fori_loop(0, 10, late, 0)
-        for stream in (4, 5, 7):
-            drained(stream, rows)
-        for stream in (6, 8, 9, 12, 13):
+        lax.fori_loop(0, steps + max(max(*v, v[0] + 2, v[1] + 2, v[4] + 3) for v in LAG_ODD), step, 0)
+        settle(4, lambda half: R - sum(is_first(half)))
+        settle(5, lambda half: R + sum(is_last(half)))
+        settle(7, lambda half: R - sum(is_last(half)))
+        for stream in (6, 8, 9):
             drained(stream, pair)
-
-        @pl.when(xl == 0)
-        def _():
-            drained(10, rows)
-            drained(11, rows)
+        settle(10, lambda half: R * (1 - half))
+        settle(11, lambda half: R * (1 - half))
+        settle(12, lambda half: sum((3 - d) * (2 - c) for c, d in zip(is_crossed(half), is_doubled(half))))
+        settle(13, lambda half: sum(is_mid(half)))
 
         @pl.when((y == 1) | (y == 2))
         def _():
-            drained(14, pair)
-            drained(15, pair)
+            settle(14, lambda half: sum(2 - c for c in is_mid(half)))
+            settle(15, lambda half: sum(2 - c for c in is_mid(half)))
 
     for copy in sent:
         copy.wait_send()
@@ -388,20 +435,22 @@
     total = width * parts
     z_size = circle // (2 * Y)
 
+    call = (mask * (genotype + 1)).astype(jnp.bfloat16)
+
     def kernel(*refs):
         exchange_kernel(z_size, *refs)
 
     sums = pl.pallas_call(
         kernel,
         out_shape=jax.ShapeDtypeStruct((rows, band), jnp.float32),
-        in_specs=[pl.BlockSpec(memory_space=pltpu.VMEM)] * 2,
+        in_specs=[pl.BlockSpec(memory_space=pltpu.VMEM)],
         out_specs=pl.BlockSpec(memory_space=pltpu.VMEM),
         scratch_shapes=[
             pltpu.VMEM((rows, width), jnp.bfloat16),
             pltpu.VMEM((SLOTS * 2 * rows, total), jnp.bfloat16),
             pltpu.VMEM((rows, total), jnp.bfloat16),
-            pltpu.VMEM((2 * Y, 8, width), jnp.float32),
-            pltpu.VMEM((z_size, 8, width), jnp.float32),
+            pltpu.VMEM((2 * Y, 8, width // 3), jnp.float32),
+            pltpu.VMEM((z_size, 8, width // 3), jnp.float32),
             pltpu.SemaphoreType.DMA((SLOTS, 2, R)),
             pltpu.SemaphoreType.DMA((4, R)),
             pltpu.SemaphoreType.DMA((4,)),
@@ -415,8 +464,8 @@
         cost_estimate=pl.CostEstimate(
             flops=2 * rows * band * total, bytes_accessed=rows * band * 4, transcendentals=0
         ),
-    )(genotype, mask)
-    return sums / total
+    )(call)
+    return sums
 
 
 def solution(mesh):

time: 135 us -> 127 us (0.941)
  Pallas kernels: 128 us -> 120 us
  other arithmetic: 4.23 us -> 1.47 us
    pallas_call x1, Pallas kernels: 128 us -> 120 us  [per_device(): pl.pallas_call(kernel, out_shape=jax.ShapeDtypeStruct((rows, band), jnp.f...]
    div x1 -> x0, other arithmetic: 4.23 us -> none  [per_device(): return sums / total]
    convert_element_type x0 -> x1, other arithmetic: none -> 1.47 us  [per_device(): call = (mask * (genotype + 1)).astype(jnp.bfloat16)]
    unnamed x4 -> x1, local copies, waits for them, and re-layouts: 2.27 us -> 3.49 us
where the time goes in v3:
time: 127 us; the launch traced here: 125 us
  Pallas kernels  120 us (94%)
  local copies, waits for them, and re-layouts  3.49 us (3%)
  other arithmetic  1.47 us (1%)
    pallas_call x1, Pallas kernels, per_device(): pl.pallas_call(kernel, out_shape=jax.ShapeDtypeStruct((rows, band), jnp.f...  120 us
    unnamed x1, local copies, waits for them, and re-layouts  3.49 us

profile of v3, /device:TPU:2, one launch (start us, length us, event | category | flops | bytes accessed | tf_op | source)
XLA Modules:
  0.0 125.4 jit_solution(15354589712803120314)
XLA Ops:
  0.0 1.5 %multiply_convert_fusion.refs_0_ = bf16[512,384]{1,0:T(8,128)(2,1)S(1)} fusion(s32[512,384]{1,0:T(8,128)} %param.3, s32[512,384]{1,0:T(8,128)} %param.2), kind=kLoop, calls=%fused_computation | loop fusion | flops 589824 | bytes 1966080 | tf_op jit(solution)/shard_map/convert_element_type | solution.py:438
  1.5 120.4 %shard_map.28 = f32[512,4224]{1,0:T(8,128)S(1)} custom-call(bf16[512,384]{1,0:T(8,128)(2,1)S(1)} %multiply_convert_fusion.refs_0_), custom_call_target="tpu_custom_call" | custom-call | flops 6643777536 | bytes 8650752 | tf_op jit(solution)/shard_map/pallas_call | solution.py:443
  121.9 3.5 %copy.4 = f32[512,4224]{1,0:T(8,128)} copy(f32[512,4224]{1,0:T(8,128)S(1)} %shard_map.28) | data formatting | bytes 17301504

commit v4 on v3

--- a/solution.py
+++ b/solution.py
@@ -10,13 +10,13 @@
 R = 16
 SLOTS = 5
 UNIT = 128
-DOUBLED = (3, 3)
+DOUBLED = (4, 3)
 CROSSED = (3, 2)
 MID_CROSSED = (0, 4)
 FIRST_DOWN = (4, 3)
-LAST_DOWN = (4, 2)
-LAG_EVEN = ((0, 2, 12), (0, 2, 15))
-LAG_ODD = ((0, 1, 4, 5, 7), (0, 2, 4, 4, 6))
+LAST_DOWN = (4, 4)
+LAG_EVEN = ((1, 3, 13), (1, 3, 16))
+LAG_ODD = ((0, 1, 2, 6, 8), (0, 2, 4, 4, 6))
 VMEM_MIB = 30
 
 
@@ -28,7 +28,7 @@
 
 def exchange_kernel(
     z_size, call, out,
-    std, slots, lhs, plane, column, recv, recv_piece, recv_lhs, recv_count, send, send_count,
+    std, slots, lhs, plane, column, recv, recv_piece, recv_row, recv_lhs, recv_count, send, send_count,
 ):
     rows, width = std.shape
     total = 4 * width
@@ -146,7 +146,7 @@
     def _():
         slots[own_rows, 0:width] = standard
 
-    for member in range(1, 4):
+    for member in range(2, 4):
         @pl.when(m == member)
         def _():
             lhs[:, member * width : (member + 1) * width] = standard
@@ -178,7 +178,6 @@
 
     mate = jnp.where(m < 2, m + 2, 5 - m)
     lhs_copy(1, std, m, mate).start()
-    pl.when(m != 1)(lambda: lhs_copy(2, std, m, 1).start())
 
     def lhs_wait(owner):
         pltpu.make_async_copy(
@@ -198,8 +197,12 @@
 
         @pl.when(m == 1)
         def _():
-            for owner in (0, 2, 3):
-                lhs_wait(owner)
+            def row_wait(r, carry):
+                row = lhs.at[pl.ds(pl.multiple_of(r * chunk, chunk), chunk)]
+                pltpu.make_async_copy(row, row, recv_row.at[r]).wait()
+                return carry
+
+            lax.fori_loop(0, R, row_wait, 0)
 
         @pl.when(m >= 2)
         def _():
@@ -260,12 +263,13 @@
                 slot = jnp.where(j == place, value, slot)
             tile(slot, jnp.where(phase < 2, mine, theirs), lax.rem(phase, 2))
 
-    def tile_step(t, early, late, whole):
-        pl.when(t == early + (R if whole else R // 2))(lhs_ready)
-        tiles_of(t - early - R // 2, (0, 4), start=int(whole))
-        if whole:
-            tiles_of(t - early - R - 2, (0, 4), stop=1)
-        tiles_of(t - late - R // 2, (1, 3, 2))
+    def tile_step(t, early, late):
+        ready = early + R
+        pl.when(t == ready)(lhs_ready)
+        tiles_of(t - early - R // 2, (0, 4), start=1)
+        tiles_of(t - ready - 2, (0, 4), stop=1)
+        tiles_of(t - late - R // 2, (1, 3, 2), start=1)
+        tiles_of(t - jnp.maximum(late + R // 2, ready + 4), (1, 3, 2), stop=1)
 
     def settle(stream, count):
         for half in range(2):
@@ -292,6 +296,14 @@
                         recv_piece.at[member, r],
                     ).wait()
                 forward(4, 0, 0, mine, r, at(0, 0, 1 - xh, m))
+                pltpu.make_async_remote_copy(
+                    src_ref=slots.at[span(0, mine, r)],
+                    dst_ref=lhs.at[pl.ds(pl.multiple_of(r * chunk, chunk), chunk)],
+                    send_sem=send.at[2],
+                    recv_sem=recv_row.at[r],
+                    device_id=at(0, 0, xh, 1),
+                    device_id_type=MESH,
+                ).start()
 
             @pl.when(jnp.logical_not(own & (xl == 0)))
             def _():
@@ -321,11 +333,12 @@
             guarded(t - lag[1], last)
             guarded(t - lag[2], sides)
             pl.when(t == 1)(pass_lhs)
-            tile_step(t, jnp.maximum(lag[0], lag[1]), lag[2], True)
+            tile_step(t, jnp.maximum(lag[0], lag[1]), lag[2])
             return carry
 
         lax.fori_loop(0, steps + max(max(v[0], v[1] + 2, v[2] + 3) for v in LAG_EVEN), step, 0)
         pl.when(xl == 0)(lambda: drained(4, rows))
+        pl.when(xl == 0)(lambda: drained(2, rows))
         settle(5, lambda half: R + sum(is_first(half)))
         settle(8, lambda half: sum(c * (3 - d) for c, d in zip(is_crossed(half), is_doubled(half))))
 
@@ -400,7 +413,7 @@
             guarded(t - lag[3], high_side)
             guarded(t - lag[4], middle)
             pl.when(t == 1)(pass_lhs)
-            tile_step(t, jnp.maximum(lag[0], lag[1]), lag[4], False)
+            tile_step(t, jnp.maximum(lag[0], lag[1]), lag[4])
             return carry
 
         lax.fori_loop(0, steps + max(max(*v, v[0] + 2, v[1] + 2, v[4] + 3) for v in LAG_ODD), step, 0)
@@ -422,7 +435,6 @@
     for copy in sent:
         copy.wait_send()
     lhs_copy(1, std, m, mate).wait_send()
-    pl.when(m != 1)(lambda: lhs_copy(2, std, m, 1).wait_send())
     pl.when(m >= 2)(lambda: lhs_copy(3, std, m - 2, 5 - m).wait_send())
     pl.when(m != 0)(lambda: pltpu.make_async_copy(std, std, send.at[0]).wait())
 
@@ -453,6 +465,7 @@
             pltpu.VMEM((z_size, 8, width // 3), jnp.float32),
             pltpu.SemaphoreType.DMA((SLOTS, 2, R)),
             pltpu.SemaphoreType.DMA((4, R)),
+            pltpu.SemaphoreType.DMA((R,)),
             pltpu.SemaphoreType.DMA((4,)),
             pltpu.SemaphoreType.DMA((2, max(z_size, 2 * Y))),
             pltpu.SemaphoreType.DMA((16,)),

time: 127 us -> 122 us (0.961)
  Pallas kernels: 120 us -> 116 us
    pallas_call x1, Pallas kernels: 120 us -> 116 us  [per_device(): pl.pallas_call(kernel, out_shape=jax.ShapeDtypeStruct((rows, band), jnp.f...]
where the time goes in v4:
time: 122 us; the launch traced here: 121 us
  Pallas kernels  116 us (95%)
  local copies, waits for them, and re-layouts  3.49 us (3%)
  other arithmetic  1.47 us (1%)
    pallas_call x1, Pallas kernels, per_device(): pl.pallas_call(kernel, out_shape=jax.ShapeDtypeStruct((rows, band), jnp.f...  116 us
    unnamed x1, local copies, waits for them, and re-layouts  3.49 us

profile of v4, /device:TPU:2, one launch (start us, length us, event | category | flops | bytes accessed | tf_op | source)
XLA Modules:
  0.0 120.6 jit_solution(7464305891487306044)
XLA Ops:
  0.0 1.5 %multiply_convert_fusion.refs_0_ = bf16[512,384]{1,0:T(8,128)(2,1)S(1)} fusion(s32[512,384]{1,0:T(8,128)} %param.3, s32[512,384]{1,0:T(8,128)} %param.2), kind=kLoop, calls=%fused_computation | loop fusion | flops 589824 | bytes 1966080 | tf_op jit(solution)/shard_map/convert_element_type | solution.py:450
  1.5 115.6 %shard_map.28 = f32[512,4224]{1,0:T(8,128)S(1)} custom-call(bf16[512,384]{1,0:T(8,128)(2,1)S(1)} %multiply_convert_fusion.refs_0_), custom_call_target="tpu_custom_call" | custom-call | flops 6643777536 | bytes 8650752 | tf_op jit(solution)/shard_map/pallas_call | solution.py:455
  117.1 3.5 %copy.4 = f32[512,4224]{1,0:T(8,128)} copy(f32[512,4224]{1,0:T(8,128)S(1)} %shard_map.28) | data formatting | bytes 17301504

commit v5 on v4

--- a/solution.py
+++ b/solution.py
@@ -11,12 +11,12 @@
 SLOTS = 5
 UNIT = 128
 DOUBLED = (4, 3)
-CROSSED = (3, 2)
+CROSSED = (2, 2)
 MID_CROSSED = (0, 4)
 FIRST_DOWN = (4, 3)
 LAST_DOWN = (4, 4)
-LAG_EVEN = ((1, 3, 13), (1, 3, 16))
-LAG_ODD = ((0, 1, 2, 6, 8), (0, 2, 4, 4, 6))
+LAG_EVEN = ((0, 2, 12), (0, 2, 15))
+LAG_ODD = ((0, 1, 2, 4, 6), (0, 2, 4, 4, 6))
 VMEM_MIB = 30
 
 

time: 122 us -> 121 us (level); the launches traced: 121 us -> 121 us
  no operation moved by 1% of the time
where the time goes in v5:
time: 121 us
  Pallas kernels  116 us (96%)
  local copies, waits for them, and re-layouts  3.49 us (3%)
  other arithmetic  1.47 us (1%)
    pallas_call x1, Pallas kernels, per_device(): pl.pallas_call(kernel, out_shape=jax.ShapeDtypeStruct((rows, band), jnp.f...  116 us
    unnamed x1, local copies, waits for them, and re-layouts  3.49 us

profile of v5, /device:TPU:2, one launch (start us, length us, event | category | flops | bytes accessed | tf_op | source)
XLA Modules:
  0.0 120.9 jit_solution(18175549769109820520)
XLA Ops:
  0.0 1.5 %multiply_convert_fusion.refs_0_ = bf16[512,384]{1,0:T(8,128)(2,1)S(1)} fusion(s32[512,384]{1,0:T(8,128)} %param.3, s32[512,384]{1,0:T(8,128)} %param.2), kind=kLoop, calls=%fused_computation | loop fusion | flops 589824 | bytes 1966080 | tf_op jit(solution)/shard_map/convert_element_type | solution.py:450
  1.5 115.9 %shard_map.28 = f32[512,4224]{1,0:T(8,128)S(1)} custom-call(bf16[512,384]{1,0:T(8,128)(2,1)S(1)} %multiply_convert_fusion.refs_0_), custom_call_target="tpu_custom_call" | custom-call | flops 6643777536 | bytes 8650752 | tf_op jit(solution)/shard_map/pallas_call | solution.py:455
  117.4 3.5 %copy.4 = f32[512,4224]{1,0:T(8,128)} copy(f32[512,4224]{1,0:T(8,128)S(1)} %shard_map.28) | data formatting | bytes 17301504
